TPU v7x, 32 devices: a whole 2x2x4 slice. The times are simulated.
32 devices in a mesh: rows: 4 (over z), cols: 4 (over y, x), space: 2 (over core).
Axes of the slice: x: 2, y: 2, z: 4, core: 2. Of those that a mesh axis runs over, the one named last changes fastest.
Arguments:
- hamiltonian: float32 [2048, 1536], P(('rows', 'cols', 'space')), may hold values from -1 to 1
- correlation_root: float32 [2048, 1536], P('rows'), may hold values from -1 to 2
- pattern: int32 [64, 48], replicated, may hold values from 0 to 1
- sub_blocks: int32 [64, 16], P(('rows', 'cols', 'space')), may hold values from 0 to 47, as said below
- sub_count: int32 [64], P(('rows', 'cols', 'space')), may hold values from 8 to 16, as said below
Outputs:
- density: float32 [2048, 1536], P(('rows', 'cols', 'space'))
- charges: float32 [2048], P(('rows', 'cols', 'space'))
Inputs may be any that keep to these rules, and one draw needn't show every extreme that they name: `sub_blocks`: row g lists distinct positions; its first entry is 16 + g mod 16, the position of block g itself. `sub_count`: some submatrix has exactly 16 live blocks.
All inputs are finite; a program needn't handle non-finite values.
Results may differ from a plain program's by a relative error of at most 0.0003.
Values sent between devices are 32-bit elements; how exact they have to be, the bound alone decides.
A program may use at most 128 MiB of HBM per device.

v0:
```python
import functools

import jax
import jax.numpy as jnp
from jax import lax
from jax.experimental import pallas as pl
from jax.experimental.pallas import tpu as pltpu
from jax.sharding import PartitionSpec as P

BLK = 32
GROUP = ("cols", "space")


def passed_along(value, axis, steps):
    count = lax.axis_size(axis)
    pairs = [(source, (source + steps) % count) for source in range(count)]
    return lax.ppermute(value, axis, pairs)


def multiply_nt(leftside, rightside):
    return lax.dot_general(
        leftside,
        rightside,
        (((1,), (1,)), ((), ())),
        precision=lax.Precision.HIGH,
        preferred_element_type=jnp.float32,
    )


def neighbour_panels(piece):
    above = passed_along(piece[1:], "rows", 1)
    below = passed_along(piece[:2], "rows", -1)
    return above, below


def window_columns(piece, above, below):
    zero = jnp.zeros(piece.shape[1:], piece.dtype)
    rows = [
        jnp.concatenate([above[0], piece[0], zero], axis=1),
        jnp.concatenate([above[1], piece[1], below[0]], axis=1),
        jnp.concatenate([zero, piece[2], below[1]], axis=1),
    ]
    return jnp.concatenate(rows, axis=0)


def split(value):
    upper = value.astype(jnp.bfloat16)
    return upper, (value - upper.astype(jnp.float32)).astype(jnp.bfloat16)


def dot_f32(leftside, rightside):
    return jnp.dot(leftside, rightside, preferred_element_type=jnp.float32)


def dot_split(leftside, rightside):
    left_hi, left_lo = leftside
    right_hi, right_lo = rightside
    return (
        dot_f32(left_hi, right_hi)
        + dot_f32(left_hi, right_lo)
        + dot_f32(left_lo, right_hi)
    )


def submatrix_kernel(maxb, slab_blocks, pos_ref, count_ref, offs_ref, gathered_ref, out_ref, rows_ref):
    width = gathered_ref.shape[2]
    slab = gathered_ref.shape[3]
    per_piece = width // BLK
    index = pl.program_id(0)
    live = count_ref[index]

    def place(p, carry):
        block = pos_ref[index, p]
        panel = block // slab_blocks
        within = lax.rem(block, slab_blocks)
        owner = within // per_piece
        start = pl.multiple_of(lax.rem(within, per_piece) * BLK, BLK)
        target = pl.multiple_of(p * BLK, BLK)
        for a in range(3):
            keep = (jnp.abs(panel - a) <= 1) & (p < live)
            values = gathered_ref[owner, 2 * panel + a, pl.ds(start, BLK), :]
            rows_ref[pl.ds(target, BLK), a * slab : (a + 1) * slab] = jnp.where(keep, values, 0.0)
        return carry

    lax.fori_loop(0, maxb, place, 0)
    offsets = offs_ref[0]
    order = maxb * BLK
    select = lax.broadcasted_iota(jnp.int32, (3 * slab, order), 0) == offsets
    select = jnp.where(select, 1.0, 0.0).astype(jnp.bfloat16)
    rows_hi, rows_lo = split(rows_ref[...])
    assembled = dot_f32(rows_hi, select) + dot_f32(rows_lo, select)
    columns = lax.broadcasted_iota(jnp.int32, (order, order), 1)
    assembled = jnp.where(columns < live * BLK, assembled, 0.0)
    symmetric = 0.5 * (assembled + assembled.T)
    total = jnp.sum(jnp.sum(symmetric * symmetric, axis=1, keepdims=True), axis=0, keepdims=True)
    live_order = jnp.full((1, 1), live * BLK, jnp.int32).astype(jnp.float32)
    iterate = symmetric * (jnp.sqrt(live_order) / (2.0 * jnp.sqrt(total + 1e-06)))
    parts = split(iterate)
    square = split(dot_split(parts, parts))
    iterate = 1.5 * iterate - 0.5 * dot_split(parts, square)
    home = iterate[:BLK]
    parts = split(iterate)
    once = dot_split((parts[0][:BLK], parts[1][:BLK]), parts)
    home = 1.5 * home - 0.5 * dot_split(split(once), parts)
    row = lax.broadcasted_iota(jnp.int32, (BLK, order), 0)
    column = lax.broadcasted_iota(jnp.int32, (BLK, order), 1)
    density = 0.5 * (jnp.where(row == column, 1.0, 0.0) - home)
    density_hi, density_lo = split(density)
    spread = functools.partial(
        lax.dot_general,
        dimension_numbers=(((1,), (1,)), ((), ())),
        preferred_element_type=jnp.float32,
    )
    out_ref[...] = spread(density_hi, select) + spread(density_lo, select)


def submatrices(gathered, sub_blocks, sub_count):
    own_blocks, maxb = sub_blocks.shape
    slab = gathered.shape[3]
    order = maxb * BLK
    offsets = sub_blocks[:, :, None] * BLK + jnp.arange(BLK, dtype=jnp.int32)
    offsets = offsets.reshape(own_blocks, 1, order)
    return pl.pallas_call(
        functools.partial(submatrix_kernel, maxb, slab // BLK),
        out_shape=jax.ShapeDtypeStruct((own_blocks * BLK, 3 * slab), jnp.float32),
        grid_spec=pltpu.PrefetchScalarGridSpec(
            num_scalar_prefetch=2,
            grid=(own_blocks,),
            in_specs=[
                pl.BlockSpec((1, 1, order), lambda i, *_: (i, 0, 0)),
                pl.BlockSpec(memory_space=pltpu.VMEM),
            ],
            out_specs=pl.BlockSpec((BLK, 3 * slab), lambda i, *_: (i, 0)),
            scratch_shapes=[pltpu.VMEM((order, 3 * slab), jnp.float32)],
        ),
    )(sub_blocks, sub_count, offsets, gathered)


def shards(hamiltonian, correlation_root, pattern, sub_blocks, sub_count):
    slab = correlation_root.shape[0]
    slab_blocks = slab // BLK
    own = hamiltonian.shape[0]
    parts = slab // own
    slab_index = lax.axis_index("rows")
    home = lax.axis_index(GROUP)
    slab_pattern = lax.dynamic_slice_in_dim(pattern, slab_index * slab_blocks, slab_blocks, 0)
    weights = slab_pattern.astype(jnp.float32)
    own_pattern = lax.dynamic_slice_in_dim(weights, home * (own // BLK), own // BLK, 0)
    own_mask = jnp.repeat(jnp.repeat(own_pattern, BLK, axis=0), BLK, axis=1)
    piece_pattern = lax.dynamic_index_in_dim(
        weights.reshape(slab_blocks, 3, parts, own // BLK), home, 2, keepdims=False
    )
    piece_mask = jnp.repeat(jnp.repeat(piece_pattern.transpose(1, 2, 0), BLK, axis=1), BLK, axis=2)

    whole_hamiltonian = lax.all_gather(hamiltonian, GROUP, axis=0, tiled=True)
    root_piece = lax.dynamic_index_in_dim(
        correlation_root.reshape(slab, 3, parts, own), home, 2, keepdims=False
    ).transpose(1, 2, 0)
    root_window = window_columns(root_piece, *neighbour_panels(root_piece))

    def step(left, window):
        return piece_mask * multiply_nt(window, left).reshape(piece_mask.shape)

    half_done = step(whole_hamiltonian, root_window)
    done_window = window_columns(half_done, *neighbour_panels(half_done))
    ortho = step(correlation_root, done_window)
    above, below = neighbour_panels(ortho)
    panels = jnp.stack([above[0], ortho[0], above[1], ortho[1], below[0], ortho[2], below[1]])
    gathered = lax.all_gather(panels, GROUP, axis=0, tiled=False)
    home_density = submatrices(gathered, sub_blocks, sub_count)
    whole_density = lax.all_gather(home_density, GROUP, axis=0, tiled=True)
    half_back = step(whole_density, root_window)
    back_window = window_columns(half_back, *neighbour_panels(half_back))
    density = multiply_nt(back_window, correlation_root).reshape(3, own, parts, own)
    density = lax.all_to_all(density.transpose(2, 3, 0, 1), GROUP, 0, 0, tiled=False)
    density = own_mask * density.transpose(1, 2, 0, 3).reshape(own, 3 * slab)
    return density, jnp.sum(density, axis=1)


def solution(mesh):
    return jax.shard_map(
        shards,
        mesh=mesh,
        in_specs=(
            P(("rows", "cols", "space"), None),
            P("rows", None),
            P(),
            P(("rows", "cols", "space"), None),
            P(("rows", "cols", "space")),
        ),
        out_specs=(P(("rows", "cols", "space"), None), P(("rows", "cols", "space"))),
        check_vma=False,
    )
```

profile of v0, /device:TPU:0, one launch (start us, length us, event | category | flops | bytes accessed | tf_op | source)
XLA Modules:
  0.0 275.0 jit_solution(14228637603605801020)
XLA Ops:
  8.0 2.4 copy.37
  10.7 3.1 %collective-permute-start = (f32[2,64,512]{1,2,0:T(8,128)S(1)}, f32[2,64,512]{1,2,0:T(8,128)S(1)}, u32[]{:S(2)}, u32[]{:S(2)}) collective-permute-start(f32[2,64,512]{1,2,0:T(8,128)S(1)} %get-tuple-element.23), channel_id=1, source_target_pairs={{0,8},{8,16},{16,24},{24,0},{1,9},{9,17},{17,25},{25,1},{2,10},{10... | collective-permute-start | bytes 786440 | tf_op jit(solution)/shard_map/ppermute | solution.py:17
  17.6 11.1 %collective-permute-done = f32[2,64,512]{1,2,0:T(8,128)S(1)} collective-permute-done((f32[2,64,512]{1,2,0:T(8,128)S(1)}, f32[2,64,512]{1,2,0:T(8,128)S(1)}, u32[]{:S(2)}, u32[]{:S(2)}) %collective-permute-start) | collective-permute-done | bytes 262176 | tf_op jit(solution)/shard_map/ppermute | solution.py:17
  28.7 9.7 %collective-permute-done.1 = f32[2,64,512]{1,2,0:T(8,128)S(1)} collective-permute-done((f32[2,64,512]{1,2,0:T(8,128)S(1)}, f32[2,64,512]{1,2,0:T(8,128)S(1)}, u32[]{:S(2)}, u32[]{:S(2)}) %collective-permute-start.1) | collective-permute-done | bytes 262176 | tf_op jit(solution)/shard_map/ppermute | solution.py:17
  38.5 6.3 %all-gather.5.cloned.1.call-done = f32[512,1536]{1,0:T(8,128)} async-done(((f32[64,1536]{1,0:T(8,128)}), f32[512,1536]{1,0:T(8,128)}) %all-gather.5.cloned.1.call-update) | async-done | bytes 3145744 | tf_op jit(solution)/shard_map/all_gather | solution.py:155
  44.8 5.1 %fusion.40 = f32[192,512]{1,0:T(8,128)S(1)} fusion(f32[512,1536]{1,0:T(8,128)} %all-gather.5.cloned.1.call-done, f32[64,512]{0,1:T(8,128)S(1)} %broadcast.22, f32[64,512]{0,1:T(8,128)S(1)} %get-tuple-element.36, f32[64,512]{0,1:T(8,128)S(1)} %get-tuple-element.21, f32[64,512]{0,1:T(8,128)S(1)} %get-tuple-element.35, f32[64,512]{0,1:T(8,128)S(1)} %copy-done.7, ...), kind=kOutput, calls=%fused_computation.81 | convolution fusion | flops 908328960 | bytes 4587520 | tf_op jit(solution)/shard_map/dot_general | solution.py:21
  52.0 2.3 collective-permute-start.3
  54.4 12.8 %collective-permute-done.2 = f32[2,64,512]{1,2,0:T(8,128)S(1)} collective-permute-done((f32[2,64,512]{1,2,0:T(8,128)S(1)}, f32[2,64,512]{1,2,0:T(8,128)S(1)}, u32[]{:S(2)}, u32[]{:S(2)}) %collective-permute-start.2) | collective-permute-done | bytes 262176 | tf_op jit(solution)/shard_map/ppermute | solution.py:17
  67.2 9.8 %collective-permute-done.3 = f32[2,64,512]{1,2,0:T(8,128)S(1)} collective-permute-done((f32[2,64,512]{1,2,0:T(8,128)S(1)}, f32[2,64,512]{1,2,0:T(8,128)S(1)}, u32[]{:S(2)}, u32[]{:S(2)}) %collective-permute-start.3) | collective-permute-done | bytes 262176 | tf_op jit(solution)/shard_map/ppermute | solution.py:17
  77.1 3.1 %fusion.4 = f32[192,512]{1,0:T(8,128)S(1)} fusion(f32[512,1536]{1,0:T(8,128)S(1)} %copy-done, f32[64,512]{0,1:T(8,128)S(1)} %copy-done.3, f32[64,512]{0,1:T(8,128)S(1)} %get-tuple-element.32, f32[64,512]{0,1:T(8,128)S(1)} %get-tuple-element.16, f32[64,512]{0,1:T(8,128)S(1)} %get-tuple-element.31, f32[64,512]{0,1:T(8,128)S(1)} %get-tuple-element.17, ...), kind=kOutput, calls=%fused_computation.10 | convolution fusion | flops 908328960 | bytes 4587520 | tf_op jit(solution)/shard_map/dot_general | solution.py:21
  83.9 2.7 collective-permute-start.5
  86.6 12.8 %collective-permute-done.4 = f32[2,64,512]{1,2,0:T(8,128)S(1)} collective-permute-done((f32[2,64,512]{1,2,0:T(8,128)S(1)}, f32[2,64,512]{1,2,0:T(8,128)S(1)}, u32[]{:S(2)}, u32[]{:S(2)}) %collective-permute-start.4) | collective-permute-done | bytes 262176 | tf_op jit(solution)/shard_map/ppermute | solution.py:17
  102.2 6.5 %collective-permute-done.5 = f32[2,64,512]{1,2,0:T(8,128)S(1)} collective-permute-done((f32[2,64,512]{1,2,0:T(8,128)S(1)}, f32[2,64,512]{1,2,0:T(8,128)S(1)}, u32[]{:S(2)}, u32[]{:S(2)}) %collective-permute-start.5) | collective-permute-done | bytes 262176 | tf_op jit(solution)/shard_map/ppermute | solution.py:17
  110.9 3.1 %copy.41 = f32[7,64,512]{2,1,0:T(8,128)} copy(f32[7,64,512]{1,2,0:T(8,128)} %slice_dynamic-update-slice_fusion) | data formatting | bytes 1835008 | tf_op jit(solution)/shard_map/stack | solution.py:168
  115.1 47.6 %all-gather.9.cloned.1.call-done = f32[56,64,512]{2,1,0:T(8,128)} async-done(((f32[7,64,512]{2,1,0:T(8,128)}), f32[56,64,512]{2,1,0:T(8,128)}) %all-gather.9.cloned.1.call-update) | async-done | bytes 7340048 | tf_op jit(solution)/shard_map/all_gather | solution.py:169
  162.7 17.8 %shard_map.68 = f32[64,1536]{1,0:T(8,128)} custom-call(s32[2,16]{1,0:T(2,128)} %pos_ref.1, s32[2]{0:T(128)} %count_ref.1, s32[2,1,512]{2,1,0:T(1,128)} %broadcast_add_fusion.offs_ref, f32[8,7,64,512]{3,2,1,0:T(8,128)} %bitcast.91), custom_call_target="tpu_custom_call" | custom-call | tf_op jit(solution)/shard_map/pallas_call | solution.py:123
  180.5 32.3 %all-gather.7.cloned.1.call-done = f32[512,1536]{1,0:T(8,128)} async-done(((f32[64,1536]{1,0:T(8,128)}), f32[512,1536]{1,0:T(8,128)}) %all-gather.7.cloned.1.call-update) | async-done | bytes 3145744 | tf_op jit(solution)/shard_map/all_gather | solution.py:171
  212.9 5.7 %fusion.38 = f32[192,512]{1,0:T(8,128)S(1)} fusion(f32[512,1536]{1,0:T(8,128)} %all-gather.7.cloned.1.call-done, f32[64,512]{0,1:T(8,128)} %copy-done.2, f32[64,512]{0,1:T(8,128)} %copy-done.11, f32[64,512]{0,1:T(8,128)} %copy-done.6, f32[64,512]{0,1:T(8,128)} %copy-done.10, f32[64,512]{0,1:T(8,128)} %get-tuple-element.22, f32[64,512]{0,1:T(8,128)} %copy-done.9, ...), kind=kOutput, calls=%fused_computation.80 | convolution fusion | flops 908328960 | bytes 4587520 | tf_op jit(solution)/shard_map/dot_general | solution.py:21
  222.6 2.3 collective-permute-start.7
  225.0 12.8 %collective-permute-done.6 = f32[2,64,512]{1,2,0:T(8,128)S(1)} collective-permute-done((f32[2,64,512]{1,2,0:T(8,128)S(1)}, f32[2,64,512]{1,2,0:T(8,128)S(1)}, u32[]{:S(2)}, u32[]{:S(2)}) %collective-permute-start.6) | collective-permute-done | bytes 262176 | tf_op jit(solution)/shard_map/ppermute | solution.py:17
  237.8 9.8 %collective-permute-done.7 = f32[2,64,512]{1,2,0:T(8,128)S(1)} collective-permute-done((f32[2,64,512]{1,2,0:T(8,128)S(1)}, f32[2,64,512]{1,2,0:T(8,128)S(1)}, u32[]{:S(2)}, u32[]{:S(2)}) %collective-permute-start.7) | collective-permute-done | bytes 262176 | tf_op jit(solution)/shard_map/ppermute | solution.py:17
  247.7 3.1 %fusion.8 = f32[192,512]{1,0:T(8,128)S(1)} fusion(f32[512,1536]{1,0:T(8,128)S(1)} %copy-done, f32[64,512]{0,1:T(8,128)S(1)} %copy-done.4, f32[64,512]{0,1:T(8,128)S(1)} %get-tuple-element.28, f32[64,512]{0,1:T(8,128)S(1)} %get-tuple-element.9, f32[64,512]{0,1:T(8,128)S(1)} %get-tuple-element.27, f32[64,512]{0,1:T(8,128)S(1)} %get-tuple-element.10, ...), kind=kOutput, calls=%fused_computation.13 | convolution fusion | flops 908328960 | bytes 4587520 | tf_op jit(solution)/shard_map/dot_general | solution.py:21
  252.4 3.5 %all-to-all-start = ((f32[8,1,12288]{2,1,0:T(1,128)}), f32[8,1,12288]{2,1,0:T(1,128)S(1)}, u32[]{:S(2)}, u32[]{:S(2)}) async-start(f32[8,1,12288]{2,1,0:T(1,128)} %reshape.88), calls=%async_computation | async-start | bytes 786432 | tf_op jit(solution)/shard_map/all_to_all | solution.py:175
  256.1 8.0 %all-to-all-done = f32[8,1,12288]{2,1,0:T(1,128)S(1)} async-done(((f32[8,1,12288]{2,1,0:T(1,128)}), f32[8,1,12288]{2,1,0:T(1,128)S(1)}, u32[]{:S(2)}, u32[]{:S(2)}) %all-to-all-start) | async-done | bytes 393248 | tf_op jit(solution)/shard_map/all_to_all | solution.py:175
  (97 shorter events, 27.1 us)
Async XLA Ops:
  7.2 37.6 %all-gather.5.cloned.1.call-start = ((), (), s32[]{:S(2)}) async-start(), calls=%async_computation.1 | async-start | bytes 3538944 | tf_op jit(solution)/shard_map/all_gather | solution.py:155
  7.9 154.8 %all-gather.9.cloned.1.call-start = ((), (), s32[]{:S(2)}) async-start(), calls=%async_computation.3 | async-start | bytes 8257536 | tf_op jit(solution)/shard_map/all_gather | solution.py:169
  10.6 6.1 %copy-start.14 = (s32[64,48]{0,1:T(8,128)S(1)}, s32[64,48]{0,1:T(8,128)}, u32[]{:S(2)}) copy-start(s32[64,48]{0,1:T(8,128)} %param.7) | copy-start | bytes 36868
  10.7 17.9 %collective-permute-start = (f32[2,64,512]{1,2,0:T(8,128)S(1)}, f32[2,64,512]{1,2,0:T(8,128)S(1)}, u32[]{:S(2)}, u32[]{:S(2)}) collective-permute-start(f32[2,64,512]{1,2,0:T(8,128)S(1)} %get-tuple-element.23), channel_id=1, source_target_pairs={{0,8},{8,16},{16,24},{24,0},{1,9},{9,17},{17,25},{25,1},{2,10},{10... | collective-permute-start | bytes 786440 | tf_op jit(solution)/shard_map/ppermute | solution.py:17
  13.8 24.6 %collective-permute-start.1 = (f32[2,64,512]{1,2,0:T(8,128)S(1)}, f32[2,64,512]{1,2,0:T(8,128)S(1)}, u32[]{:S(2)}, u32[]{:S(2)}) collective-permute-start(f32[2,64,512]{1,2,0:T(8,128)S(1)} %get-tuple-element.24), channel_id=1, source_target_pairs={{0,24},{8,0},{16,8},{24,16},{1,25},{9,1},{17,9},{25,17},{2,26},{10... | collective-permute-start | bytes 786440 | tf_op jit(solution)/shard_map/ppermute | solution.py:17
  16.7 33.3 %copy-start.5 = (f32[64,512]{0,1:T(8,128)}, f32[64,512]{0,1:T(8,128)S(1)}, u32[]{:S(2)}) copy-start(f32[64,512]{0,1:T(8,128)S(1)} %get-tuple-element.20) | copy-start | bytes 393220
  16.7 33.3 %copy-start.6 = (f32[64,512]{0,1:T(8,128)}, f32[64,512]{0,1:T(8,128)S(1)}, u32[]{:S(2)}) copy-start(f32[64,512]{0,1:T(8,128)S(1)} %get-tuple-element.21) | copy-start | bytes 393220
  16.7 28.1 %copy-start.7 = (f32[64,512]{0,1:T(8,128)S(1)}, f32[64,512]{0,1:T(8,128)}, u32[]{:S(2)}) copy-start(f32[64,512]{0,1:T(8,128)} %get-tuple-element.22) | copy-start | bytes 393220
  17.6 32.7 %copy-start.1 = (f32[3,64,16]{1,2,0:T(8,128)}, f32[3,64,16]{1,2,0:T(8,128)S(1)}, u32[]{:S(2)}) copy-start(f32[3,64,16]{1,2,0:T(8,128)S(1)} %reshape.79) | copy-start | bytes 36868
  28.7 21.3 %copy-start.8 = (f32[64,512]{0,1:T(8,128)}, f32[64,512]{0,1:T(8,128)S(1)}, u32[]{:S(2)}) copy-start(f32[64,512]{0,1:T(8,128)S(1)} %get-tuple-element.33) | copy-start | bytes 393220
  28.7 21.3 %copy-start.9 = (f32[64,512]{0,1:T(8,128)}, f32[64,512]{0,1:T(8,128)S(1)}, u32[]{:S(2)}) copy-start(f32[64,512]{0,1:T(8,128)S(1)} %get-tuple-element.34) | copy-start | bytes 393220
  38.5 11.5 %copy-start.10 = (f32[64,512]{0,1:T(8,128)}, f32[64,512]{0,1:T(8,128)S(1)}, u32[]{:S(2)}) copy-start(f32[64,512]{0,1:T(8,128)S(1)} %get-tuple-element.35) | copy-start | bytes 393220
  38.5 11.5 %copy-start.11 = (f32[64,512]{0,1:T(8,128)}, f32[64,512]{0,1:T(8,128)S(1)}, u32[]{:S(2)}) copy-start(f32[64,512]{0,1:T(8,128)S(1)} %get-tuple-element.36) | copy-start | bytes 393220
  50.5 16.7 %collective-permute-start.2 = (f32[2,64,512]{1,2,0:T(8,128)S(1)}, f32[2,64,512]{1,2,0:T(8,128)S(1)}, u32[]{:S(2)}, u32[]{:S(2)}) collective-permute-start(f32[2,64,512]{1,2,0:T(8,128)S(1)} %get-tuple-element.18), channel_id=1, source_target_pairs={{0,8},{8,16},{16,24},{24,0},{1,9},{9,17},{17,25},{25,1},{2,10},{10... | collective-permute-start | bytes 786440 | tf_op jit(solution)/shard_map/ppermute | solution.py:17
  52.0 25.1 %copy-start = (f32[512,1536]{1,0:T(8,128)S(1)}, f32[512,1536]{1,0:T(8,128)}, u32[]{:S(2)}) copy-start(f32[512,1536]{1,0:T(8,128)} %param.6) | copy-start | bytes 9437188
  52.0 25.1 %copy-start.3 = (f32[64,512]{0,1:T(8,128)S(1)}, f32[64,512]{0,1:T(8,128)}, u32[]{:S(2)}) copy-start(f32[64,512]{0,1:T(8,128)} %copy-done.2) | copy-start | bytes 393220
  52.0 25.0 %collective-permute-start.3 = (f32[2,64,512]{1,2,0:T(8,128)S(1)}, f32[2,64,512]{1,2,0:T(8,128)S(1)}, u32[]{:S(2)}, u32[]{:S(2)}) collective-permute-start(f32[2,64,512]{1,2,0:T(8,128)S(1)} %get-tuple-element.19), channel_id=1, source_target_pairs={{0,24},{8,0},{16,8},{24,16},{1,25},{9,1},{17,9},{25,17},{2,26},{10... | collective-permute-start | bytes 786440 | tf_op jit(solution)/shard_map/ppermute | solution.py:17
  82.7 16.7 %collective-permute-start.4 = (f32[2,64,512]{1,2,0:T(8,128)S(1)}, f32[2,64,512]{1,2,0:T(8,128)S(1)}, u32[]{:S(2)}, u32[]{:S(2)}) collective-permute-start(f32[2,64,512]{1,2,0:T(8,128)S(1)} %get-tuple-element.14), channel_id=1, source_target_pairs={{0,8},{8,16},{16,24},{24,0},{1,9},{9,17},{17,25},{25,1},{2,10},{10... | collective-permute-start | bytes 786440 | tf_op jit(solution)/shard_map/ppermute | solution.py:17
  83.9 24.8 %collective-permute-start.5 = (f32[2,64,512]{1,2,0:T(8,128)S(1)}, f32[2,64,512]{1,2,0:T(8,128)S(1)}, u32[]{:S(2)}, u32[]{:S(2)}) collective-permute-start(f32[2,64,512]{1,2,0:T(8,128)S(1)} %get-tuple-element.13), channel_id=1, source_target_pairs={{0,24},{8,0},{16,8},{24,16},{1,25},{9,1},{17,9},{25,17},{2,26},{10... | collective-permute-start | bytes 786440 | tf_op jit(solution)/shard_map/ppermute | solution.py:17
  114.0 98.9 %all-gather.7.cloned.1.call-start = ((), (), s32[]{:S(2)}) async-start(), calls=%async_computation.2 | async-start | bytes 3538944 | tf_op jit(solution)/shard_map/all_gather | solution.py:171
  221.1 16.7 %collective-permute-start.6 = (f32[2,64,512]{1,2,0:T(8,128)S(1)}, f32[2,64,512]{1,2,0:T(8,128)S(1)}, u32[]{:S(2)}, u32[]{:S(2)}) collective-permute-start(f32[2,64,512]{1,2,0:T(8,128)S(1)} %get-tuple-element.11), channel_id=1, source_target_pairs={{0,8},{8,16},{16,24},{24,0},{1,9},{9,17},{17,25},{25,1},{2,10},{10... | collective-permute-start | bytes 786440 | tf_op jit(solution)/shard_map/ppermute | solution.py:17
  222.6 25.1 %copy-start.4 = (f32[64,512]{0,1:T(8,128)S(1)}, f32[64,512]{0,1:T(8,128)}, u32[]{:S(2)}) copy-start(f32[64,512]{0,1:T(8,128)} %copy-done.2) | copy-start | bytes 393220
  222.6 25.0 %collective-permute-start.7 = (f32[2,64,512]{1,2,0:T(8,128)S(1)}, f32[2,64,512]{1,2,0:T(8,128)S(1)}, u32[]{:S(2)}, u32[]{:S(2)}) collective-permute-start(f32[2,64,512]{1,2,0:T(8,128)S(1)} %get-tuple-element.12), channel_id=1, source_target_pairs={{0,24},{8,0},{16,8},{24,16},{1,25},{9,1},{17,9},{25,17},{2,26},{10... | collective-permute-start | bytes 786440 | tf_op jit(solution)/shard_map/ppermute | solution.py:17
  252.4 11.7 %all-to-all-start = ((f32[8,1,12288]{2,1,0:T(1,128)}), f32[8,1,12288]{2,1,0:T(1,128)S(1)}, u32[]{:S(2)}, u32[]{:S(2)}) async-start(f32[8,1,12288]{2,1,0:T(1,128)} %reshape.88), calls=%async_computation | async-start | bytes 786432 | tf_op jit(solution)/shard_map/all_to_all | solution.py:175
  (4 other events, 14.0 us)
Sparse Core Ops, SparseCore 0:
  9.9 34.8 all-gather.4
  114.1 48.5 all-gather.8
  180.7 32.1 all-gather.6
where the time goes:
time: 275 us
  waiting for transfers between devices  180 us (65%)
  starting transfers between devices  20.6 us (7%)
  local copies, waits for them, and re-layouts  19.6 us (7%)
  Pallas kernels  17.8 us (6%)
  matrix products  17.2 us (6%)
  between operations  14.2 us (5%)
  other arithmetic  5.51 us (2%)
    ppermute x8, waiting for transfers between devices, passed_along(): return lax.ppermute(value, axis, pairs)  85.2 us
    all_gather x1, waiting for transfers between devices, shards(): gathered = lax.all_gather(panels, GROUP, axis=0, tiled=False)  47.6 us
    all_gather x1, waiting for transfers between devices, shards(): whole_density = lax.all_gather(home_density, GROUP, axis=0, tiled=True)  32.3 us
    pallas_call x1, Pallas kernels, submatrices(): pl.pallas_call(functools.partial(submatrix_kernel, maxb, slab // BLK), ou...  17.8 us
    dot_general x4, matrix products, multiply_nt(): lax.dot_general(leftside, rightside, (((1,), (1,)), ((), ())), precision=...  17.2 us
    ppermute x8, starting transfers between devices, passed_along(): return lax.ppermute(value, axis, pairs)  16.8 us
    unnamed x42, local copies, waits for them, and re-layouts  9.82 us
    all_to_all x1, waiting for transfers between devices, shards(): lax.all_to_all(density.transpose(2, 3, 0, 1), GROUP, 0, 0, tiled=False)  8 us
  transfers between devices with their start and end apart: 12, of which 12 were waited for; matrix products, arithmetic and copies ran while one was open for 3% of the time, Pallas kernels for 0%

commit v1 on v0

--- a/solution.py
+++ b/solution.py
@@ -9,12 +9,6 @@
 
 BLK = 32
 GROUP = ("cols", "space")
-
-
-def passed_along(value, axis, steps):
-    count = lax.axis_size(axis)
-    pairs = [(source, (source + steps) % count) for source in range(count)]
-    return lax.ppermute(value, axis, pairs)
 
 
 def multiply_nt(leftside, rightside):
@@ -27,20 +21,196 @@
     )
 
 
-def neighbour_panels(piece):
-    above = passed_along(piece[1:], "rows", 1)
-    below = passed_along(piece[:2], "rows", -1)
+class Sender:
+    def __init__(self, send_sems, recv_sems):
+        self.sems = (send_sems, recv_sems)
+        self.copies = []
+
+    def start(self, source, target, device):
+        slot = len(self.copies)
+        copy = pltpu.make_async_remote_copy(
+            src_ref=source,
+            dst_ref=target,
+            send_sem=self.sems[0].at[slot],
+            recv_sem=self.sems[1].at[slot],
+            device_id=device,
+            device_id_type=pl.DeviceIdType.MESH,
+        )
+        copy.start()
+        self.copies.append(copy)
+        return copy
+
+    def finish(self):
+        for copy in self.copies:
+            copy.wait_send()
+
+
+class Gather:
+    def __init__(self, sender, source, out_ref, rows, lanes):
+        self.sender, self.out_ref, self.rows, self.lanes = sender, out_ref, rows, lanes
+        col = lax.axis_index("cols")
+        space = lax.axis_index("space")
+        self.first = col + 1 - 2 * lax.rem(col, 2)
+        self.second = lax.rem(col + 2, 4)
+        self.third = lax.rem(self.first + 2, 4)
+        self.space = space
+        own = self.region(col)
+        self.from_first = sender.start(source, own, {"cols": self.first})
+        self.from_second = sender.start(source, own, {"cols": self.second})
+        self.pending = [sender.start(source, own, {"space": 1 - space})]
+
+    def region(self, col, half=None):
+        start, size = self.rows
+        if half is not None:
+            size = size // 2
+            start = start + half * size
+        owner = col * 2 + self.space
+        return self.out_ref.at[owner, pl.ds(start, size), pl.ds(*self.lanes)]
+
+    def partner(self, region):
+        self.pending.append(self.sender.start(region, region, {"space": 1 - self.space}))
+
+    def relay(self):
+        self.from_first.wait_recv()
+        passed = self.region(self.first, 1)
+        self.half_second = self.sender.start(passed, passed, {"cols": self.second})
+        self.partner(self.region(self.first))
+        self.from_second.wait_recv()
+        passed = self.region(self.second, 0)
+        self.half_first = self.sender.start(passed, passed, {"cols": self.first})
+        self.partner(self.region(self.second))
+
+    def last_hop(self):
+        self.half_second.wait_recv()
+        self.partner(self.region(self.third, 1))
+        self.half_first.wait_recv()
+        self.partner(self.region(self.third, 0))
+
+    def finish(self):
+        for copy in self.pending:
+            copy.wait_recv()
+
+
+def meet(along_rows, in_slab):
+    barrier = pltpu.get_barrier_semaphore()
+    devices = []
+    if along_rows:
+        row = lax.axis_index("rows")
+        count = lax.axis_size("rows")
+        devices += [{"rows": lax.rem(row + 1, count)}, {"rows": lax.rem(row + count - 1, count)}]
+    if in_slab:
+        col = lax.axis_index("cols")
+        devices += [{"cols": col + 1 - 2 * lax.rem(col, 2)}, {"cols": lax.rem(col + 2, 4)}]
+        devices += [{"space": 1 - lax.axis_index("space")}]
+    for device in devices:
+        pl.semaphore_signal(barrier, inc=1, device_id=device, device_id_type=pl.DeviceIdType.MESH)
+    pl.semaphore_wait(barrier, len(devices))
+
+
+def send_panels(sender, piece_ref, window_ref):
+    row = lax.axis_index("rows")
+    count = lax.axis_size("rows")
+    height, slab = piece_ref.shape
+    own = height // 3
+    above = sender.start(
+        piece_ref.at[pl.ds(own, 2 * own), :],
+        window_ref.at[pl.ds(0, 2 * own), pl.ds(0, slab)],
+        {"rows": lax.rem(row + 1, count)},
+    )
+    below = sender.start(
+        piece_ref.at[pl.ds(0, 2 * own), :],
+        window_ref.at[pl.ds(own, 2 * own), pl.ds(2 * slab, slab)],
+        {"rows": lax.rem(row + count - 1, count)},
+    )
     return above, below
 
 
-def window_columns(piece, above, below):
-    zero = jnp.zeros(piece.shape[1:], piece.dtype)
-    rows = [
-        jnp.concatenate([above[0], piece[0], zero], axis=1),
-        jnp.concatenate([above[1], piece[1], below[0]], axis=1),
-        jnp.concatenate([zero, piece[2], below[1]], axis=1),
-    ]
-    return jnp.concatenate(rows, axis=0)
+def fill_rest(piece_ref, window_ref, slab, own):
+    zero = jnp.zeros((own, slab), jnp.float32)
+    window_ref[2 * own :, :slab] = zero
+    window_ref[:own, 2 * slab :] = zero
+
+
+def exchange_kernel(piece_ref, window_ref, send_sems, recv_sems):
+    meet(True, False)
+    sender = Sender(send_sems, recv_sems)
+    copies = send_panels(sender, piece_ref, window_ref)
+    height, slab = piece_ref.shape
+    window_ref[:, slab : 2 * slab] = piece_ref[...]
+    fill_rest(piece_ref, window_ref, slab, height // 3)
+    for copy in copies:
+        copy.wait_recv()
+    sender.finish()
+
+
+def gather_kernel(block_ref, out_ref, send_sems, recv_sems):
+    meet(False, True)
+    sender = Sender(send_sems, recv_sems)
+    height, width = block_ref.shape
+    gather = Gather(sender, block_ref, out_ref, (0, height), (0, width))
+    out_ref[lax.axis_index(GROUP)] = block_ref[...]
+    gather.relay()
+    gather.last_hop()
+    gather.finish()
+    sender.finish()
+
+
+def both_kernel(piece_ref, block_ref, window_ref, out_ref, send_sems, recv_sems):
+    meet(True, True)
+    sender = Sender(send_sems, recv_sems)
+    copies = send_panels(sender, piece_ref, window_ref)
+    height, width = block_ref.shape
+    gather = Gather(sender, block_ref, out_ref, (0, height), (0, width))
+    out_ref[lax.axis_index(GROUP)] = block_ref[...]
+    height, slab = piece_ref.shape
+    window_ref[:, slab : 2 * slab] = piece_ref[...]
+    fill_rest(piece_ref, window_ref, slab, height // 3)
+    gather.relay()
+    gather.last_hop()
+    gather.finish()
+    for copy in copies:
+        copy.wait_recv()
+    sender.finish()
+
+
+def window_kernel(piece_ref, out_ref, send_sems, recv_sems):
+    meet(True, True)
+    sender = Sender(send_sems, recv_sems)
+    height, slab = piece_ref.shape
+    own = height // 3
+    home = lax.axis_index(GROUP)
+    above, below = send_panels(sender, piece_ref, out_ref.at[home])
+    gathers = [Gather(sender, piece_ref, out_ref, (0, height), (slab, slab))]
+    out_ref[home, :, slab : 2 * slab] = piece_ref[...]
+    zero = jnp.zeros((own, slab), jnp.float32)
+    for owner in range(out_ref.shape[0]):
+        out_ref[owner, 2 * own :, :slab] = zero
+        out_ref[owner, :own, 2 * slab :] = zero
+    for copy, start, lane in ((above, 0, 0), (below, own, 2 * slab)):
+        copy.wait_recv()
+        source = out_ref.at[home, pl.ds(start, 2 * own), pl.ds(lane, slab)]
+        gathers.append(Gather(sender, source, out_ref, (start, 2 * own), (lane, slab)))
+    for gather in gathers:
+        gather.relay()
+    for gather in gathers:
+        gather.last_hop()
+    for gather in gathers:
+        gather.finish()
+    sender.finish()
+
+
+def exchange_call(kernel, copies, collective, shapes, *operands):
+    space = pl.BlockSpec(memory_space=pltpu.VMEM)
+    return pl.pallas_call(
+        kernel,
+        out_shape=[jax.ShapeDtypeStruct(shape, jnp.float32) for shape in shapes],
+        in_specs=[space] * len(operands),
+        out_specs=[space] * len(shapes),
+        scratch_shapes=[pltpu.SemaphoreType.DMA((copies,)), pltpu.SemaphoreType.DMA((copies,))],
+        compiler_params=pltpu.CompilerParams(
+            collective_id=collective, has_side_effects=True, vmem_limit_bytes=40 * 2**20
+        ),
+    )(*operands)
 
 
 def split(value):
@@ -63,8 +233,8 @@
 
 
 def submatrix_kernel(maxb, slab_blocks, pos_ref, count_ref, offs_ref, gathered_ref, out_ref, rows_ref):
-    width = gathered_ref.shape[2]
-    slab = gathered_ref.shape[3]
+    width = gathered_ref.shape[1] // 3
+    slab = gathered_ref.shape[2] // 3
     per_piece = width // BLK
     index = pl.program_id(0)
     live = count_ref[index]
@@ -74,12 +244,10 @@
         panel = block // slab_blocks
         within = lax.rem(block, slab_blocks)
         owner = within // per_piece
-        start = pl.multiple_of(lax.rem(within, per_piece) * BLK, BLK)
+        start = pl.multiple_of(panel * width + lax.rem(within, per_piece) * BLK, BLK)
         target = pl.multiple_of(p * BLK, BLK)
-        for a in range(3):
-            keep = (jnp.abs(panel - a) <= 1) & (p < live)
-            values = gathered_ref[owner, 2 * panel + a, pl.ds(start, BLK), :]
-            rows_ref[pl.ds(target, BLK), a * slab : (a + 1) * slab] = jnp.where(keep, values, 0.0)
+        values = gathered_ref[owner, pl.ds(start, BLK), :]
+        rows_ref[pl.ds(target, BLK), :] = jnp.where(p < live, values, 0.0)
         return carry
 
     lax.fori_loop(0, maxb, place, 0)
@@ -116,7 +284,7 @@
 
 def submatrices(gathered, sub_blocks, sub_count):
     own_blocks, maxb = sub_blocks.shape
-    slab = gathered.shape[3]
+    slab = gathered.shape[2] // 3
     order = maxb * BLK
     offsets = sub_blocks[:, :, None] * BLK + jnp.arange(BLK, dtype=jnp.int32)
     offsets = offsets.reshape(own_blocks, 1, order)
@@ -151,26 +319,28 @@
         weights.reshape(slab_blocks, 3, parts, own // BLK), home, 2, keepdims=False
     )
     piece_mask = jnp.repeat(jnp.repeat(piece_pattern.transpose(1, 2, 0), BLK, axis=1), BLK, axis=2)
-
-    whole_hamiltonian = lax.all_gather(hamiltonian, GROUP, axis=0, tiled=True)
+    piece_mask = piece_mask.reshape(3 * own, slab)
+
     root_piece = lax.dynamic_index_in_dim(
         correlation_root.reshape(slab, 3, parts, own), home, 2, keepdims=False
-    ).transpose(1, 2, 0)
-    root_window = window_columns(root_piece, *neighbour_panels(root_piece))
+    ).transpose(1, 2, 0).reshape(3 * own, slab)
+    window_shape = (3 * own, 3 * slab)
+    block_shape = (parts, own, 3 * slab)
+    root_window, whole_hamiltonian = exchange_call(
+        both_kernel, 11, 1, [window_shape, block_shape], root_piece, hamiltonian
+    )
 
     def step(left, window):
-        return piece_mask * multiply_nt(window, left).reshape(piece_mask.shape)
+        return piece_mask * multiply_nt(window, left.reshape(slab, 3 * slab))
 
     half_done = step(whole_hamiltonian, root_window)
-    done_window = window_columns(half_done, *neighbour_panels(half_done))
+    (done_window,) = exchange_call(exchange_kernel, 2, 2, [window_shape], half_done)
     ortho = step(correlation_root, done_window)
-    above, below = neighbour_panels(ortho)
-    panels = jnp.stack([above[0], ortho[0], above[1], ortho[1], below[0], ortho[2], below[1]])
-    gathered = lax.all_gather(panels, GROUP, axis=0, tiled=False)
+    (gathered,) = exchange_call(window_kernel, 29, 3, [(parts, *window_shape)], ortho)
     home_density = submatrices(gathered, sub_blocks, sub_count)
-    whole_density = lax.all_gather(home_density, GROUP, axis=0, tiled=True)
+    (whole_density,) = exchange_call(gather_kernel, 9, 4, [block_shape], home_density)
     half_back = step(whole_density, root_window)
-    back_window = window_columns(half_back, *neighbour_panels(half_back))
+    (back_window,) = exchange_call(exchange_kernel, 2, 5, [window_shape], half_back)
     density = multiply_nt(back_window, correlation_root).reshape(3, own, parts, own)
     density = lax.all_to_all(density.transpose(2, 3, 0, 1), GROUP, 0, 0, tiled=False)
     density = own_mask * density.transpose(1, 2, 0, 3).reshape(own, 3 * slab)

time: 275 us -> 161 us (0.59)
  waiting for transfers between devices: 180 us -> 8.01 us
  Pallas kernels: 17.8 us -> 124 us
  starting transfers between devices: 20.6 us -> 3.45 us
  between operations: 14.2 us -> 0.88 us
  matrix products: 17.2 us -> 6.8 us
  local copies, waits for them, and re-layouts: 19.6 us -> 14.4 us
    pallas_call x0 -> x5, Pallas kernels: none -> 105 us  [exchange_call(): pl.pallas_call(kernel, out_shape=[jax.ShapeDtypeStruct(shape, jnp.float32...]
    all_gather x3 -> x0, waiting for transfers between devices: 86.2 us -> none  [the longest x1 47.6 us: shards(): gathered = lax.all_gather(panels, GROUP, axis=0, tiled=False)]
    ppermute x8 -> x0, waiting for transfers between devices: 85.2 us -> none  [passed_along(): return lax.ppermute(value, axis, pairs)]
    ppermute x8 -> x0, starting transfers between devices: 16.8 us -> none  [passed_along(): return lax.ppermute(value, axis, pairs)]
    dot_general x4, matrix products: 17.2 us -> 6.8 us  [multiply_nt(): lax.dot_general(leftside, rightside, (((1,), (1,)), ((), ())), precision=...]
    another operation x3 -> x2, local copies, waits for them, and re-layouts: 3.8 us -> 0.74 us  [shards(): piece_mask = piece_mask.reshape(3 * own, slab)]
    unnamed x42 -> x16, local copies, waits for them, and re-layouts: 9.82 us -> 10.8 us
  transfers between devices with their start and end apart: 12 -> 1, of which waited for: 12 -> 1; matrix products, arithmetic and copies ran while one was open for 3% -> 0% of each run, Pallas kernels for 0% -> 0%
where the time goes in v1:
time: 161 us
  Pallas kernels  124 us (77%)
  local copies, waits for them, and re-layouts  14.4 us (9%)
  waiting for transfers between devices  8.01 us (5%)
  matrix products  6.8 us (4%)
  other arithmetic  3.81 us (2%)
  starting transfers between devices  3.45 us (2%)
    pallas_call x5, Pallas kernels, exchange_call(): pl.pallas_call(kernel, out_shape=[jax.ShapeDtypeStruct(shape, jnp.float32...  105 us
    pallas_call x1, Pallas kernels, submatrices(): pl.pallas_call(functools.partial(submatrix_kernel, maxb, slab // BLK), ou...  18.4 us
    unnamed x16, local copies, waits for them, and re-layouts  10.8 us
    all_to_all x1, waiting for transfers between devices, shards(): lax.all_to_all(density.transpose(2, 3, 0, 1), GROUP, 0, 0, tiled=False)  8.01 us
    dot_general x4, matrix products, multiply_nt(): lax.dot_general(leftside, rightside, (((1,), (1,)), ((), ())), precision=...  6.8 us
    all_to_all x1, starting transfers between devices, shards(): lax.all_to_all(density.transpose(2, 3, 0, 1), GROUP, 0, 0, tiled=False)  3.45 us
  transfers between devices with their start and end apart: 1, of which 1 were waited for; matrix products, arithmetic and copies ran while one was open for 0% of the time, Pallas kernels for 0%

profile of v1, /device:TPU:0, one launch (start us, length us, event | category | flops | bytes accessed | tf_op | source)
XLA Modules:
  0.0 160.8 jit_solution(14152988122888022578)
XLA Ops:
  0.6 0.8 dynamic-slice_convert_fusion
  1.9 0.6 reshape_reshape.3
  2.7 3.6 %copy.35 = f32[512,1536]{0,1:T(8,128)} copy(f32[512,1536]{1,0:T(8,128)} %param.6) | data formatting | bytes 6291456 | tf_op args[1]
  6.3 1.0 constant_dynamic-slice_fusion
  7.3 22.5 %shard_map.68 = (f32[192,1536]{1,0:T(8,128)S(1)}, f32[8,64,1536]{2,1,0:T(8,128)S(1)}) custom-call(f32[192,512]{1,0:T(8,128)S(1)} %bitcast.51, f32[64,1536]{1,0:T(8,128)S(1)} %copy-done.2), custom_call_target="tpu_custom_call" | custom-call | tf_op jit(solution)/shard_map/pallas_call | solution.py:204
  29.9 1.7 %convolution_multiply_fusion.2.piece_ref = f32[192,512]{1,0:T(8,128)S(1)} fusion(f32[192,512]{1,0:T(8,128)S(1)} %copy.38, f32[192,1536]{1,0:T(8,128)S(1)} %get-tuple-element.4, f32[512,1536]{1,0:T(8,128)S(1)} %bitcast.50), kind=kOutput, calls=%fused_computation.2 | convolution fusion | flops 906067968 | bytes 5111808 | tf_op jit(solution)/shard_map/dot_general | solution.py:15
  31.6 14.3 %shard_map.69 = f32[192,1536]{1,0:T(8,128)S(1)} custom-call(f32[192,512]{1,0:T(8,128)S(1)} %convolution_multiply_fusion.2.piece_ref), custom_call_target="tpu_custom_call" | custom-call | tf_op jit(solution)/shard_map/pallas_call | solution.py:204
  45.9 1.7 %convolution_multiply_fusion.1.piece_ref = f32[192,512]{1,0:T(8,128)S(1)} fusion(f32[192,512]{1,0:T(8,128)S(1)} %copy.38, f32[192,1536]{1,0:T(8,128)S(1)} %shard_map.69, f32[512,1536]{1,0:T(8,128)S(1)} %copy-done.3), kind=kOutput, calls=%fused_computation.1 | convolution fusion | flops 906067968 | bytes 5111808 | tf_op jit(solution)/shard_map/dot_general | solution.py:15
  47.6 35.1 %shard_map.70.gathered_ref = f32[8,192,1536]{2,1,0:T(8,128)S(1)} custom-call(f32[192,512]{1,0:T(8,128)S(1)} %convolution_multiply_fusion.1.piece_ref), custom_call_target="tpu_custom_call" | custom-call | tf_op jit(solution)/shard_map/pallas_call | solution.py:204
  82.7 3.6 %copy-done = f32[8,192,1536]{2,1,0:T(8,128)} copy-done((f32[8,192,1536]{2,1,0:T(8,128)}, f32[8,192,1536]{2,1,0:T(8,128)S(1)}, u32[]{:S(2)}) %copy-start) | copy-done | bytes 9437208
  86.6 0.6 broadcast_add_fusion.offs_ref
  87.2 18.4 %shard_map.71.block_ref = f32[64,1536]{1,0:T(8,128)} custom-call(s32[2,16]{1,0:T(2,128)} %pos_ref.1, s32[2]{0:T(128)} %count_ref.1, s32[2,1,512]{2,1,0:T(1,128)} %broadcast_add_fusion.offs_ref, f32[8,192,1536]{2,1,0:T(8,128)} %copy-done), custom_call_target="tpu_custom_call" | custom-call | tf_op jit(solution)/shard_map/pallas_call | solution.py:291
  105.6 1.0 copy-done.1
  106.6 19.0 %shard_map.72 = f32[8,64,1536]{2,1,0:T(8,128)S(1)} custom-call(f32[64,1536]{1,0:T(8,128)S(1)} %copy-done.1), custom_call_target="tpu_custom_call" | custom-call | tf_op jit(solution)/shard_map/pallas_call | solution.py:204
  125.5 1.7 %convolution_multiply_fusion.piece_ref = f32[192,512]{1,0:T(8,128)S(1)} fusion(f32[192,512]{1,0:T(8,128)S(1)} %copy.38, f32[192,1536]{1,0:T(8,128)S(1)} %get-tuple-element.4, f32[512,1536]{1,0:T(8,128)S(1)} %bitcast.49), kind=kOutput, calls=%fused_computation | convolution fusion | flops 906067968 | bytes 5111808 | tf_op jit(solution)/shard_map/dot_general | solution.py:15
  127.2 14.3 %shard_map.73 = f32[192,1536]{1,0:T(8,128)S(1)} custom-call(f32[192,512]{1,0:T(8,128)S(1)} %convolution_multiply_fusion.piece_ref), custom_call_target="tpu_custom_call" | custom-call | tf_op jit(solution)/shard_map/pallas_call | solution.py:204
  141.5 1.7 %fusion.2 = f32[192,512]{1,0:T(8,128)S(1)} fusion(f32[192,1536]{1,0:T(8,128)S(1)} %shard_map.73, f32[512,1536]{1,0:T(8,128)S(1)} %copy-done.4), kind=kOutput, calls=%fused_computation.14 | convolution fusion | flops 905969664 | bytes 4718592 | tf_op jit(solution)/shard_map/dot_general | solution.py:15
  143.6 1.2 reshape.83
  144.8 3.5 %all-to-all-start = ((f32[8,1,12288]{2,1,0:T(1,128)}), f32[8,1,12288]{2,1,0:T(1,128)S(1)}, u32[]{:S(2)}, u32[]{:S(2)}) async-start(f32[8,1,12288]{2,1,0:T(1,128)} %reshape.83), calls=%async_computation | async-start | bytes 786432 | tf_op jit(solution)/shard_map/all_to_all | solution.py:345
  148.5 8.0 %all-to-all-done = f32[8,1,12288]{2,1,0:T(1,128)S(1)} async-done(((f32[8,1,12288]{2,1,0:T(1,128)}), f32[8,1,12288]{2,1,0:T(1,128)S(1)}, u32[]{:S(2)}, u32[]{:S(2)}) %all-to-all-start) | async-done | bytes 393248 | tf_op jit(solution)/shard_map/all_to_all | solution.py:345
  156.5 0.5 broadcast.19
  157.0 1.6 reduce.2
  159.0 1.0 copy.41
  160.1 0.8 fusion
  (32 shorter events, 1.9 us)
Async XLA Ops:
  2.7 4.6 %copy-start.2 = (f32[64,1536]{1,0:T(8,128)S(1)}, f32[64,1536]{1,0:T(8,128)}, u32[]{:S(2)}) copy-start(f32[64,1536]{1,0:T(8,128)} %block_ref.1) | copy-start | bytes 1179652
  29.9 16.0 %copy-start.3 = (f32[512,1536]{1,0:T(8,128)S(1)}, f32[512,1536]{1,0:T(8,128)}, u32[]{:S(2)}) copy-start(f32[512,1536]{1,0:T(8,128)} %param.6) | copy-start | bytes 9437188
  47.6 38.8 %copy-start.5 = (s32[2,16]{1,0:T(2,128)S(1)}, s32[2,16]{1,0:T(2,128)}, u32[]{:S(2)}) copy-start(s32[2,16]{1,0:T(2,128)} %pos_ref.1) | copy-start | bytes 388
  82.7 3.6 %copy-start = (f32[8,192,1536]{2,1,0:T(8,128)}, f32[8,192,1536]{2,1,0:T(8,128)S(1)}, u32[]{:S(2)}) copy-start(f32[8,192,1536]{2,1,0:T(8,128)S(1)} %shard_map.70.gathered_ref) | copy-start | bytes 28311556
  105.6 1.0 copy-start.1
  125.5 16.0 %copy-start.4 = (f32[512,1536]{1,0:T(8,128)S(1)}, f32[512,1536]{1,0:T(8,128)}, u32[]{:S(2)}) copy-start(f32[512,1536]{1,0:T(8,128)} %param.6) | copy-start | bytes 9437188
  144.8 11.7 %all-to-all-start = ((f32[8,1,12288]{2,1,0:T(1,128)}), f32[8,1,12288]{2,1,0:T(1,128)S(1)}, u32[]{:S(2)}, u32[]{:S(2)}) async-start(f32[8,1,12288]{2,1,0:T(1,128)} %reshape.83), calls=%async_computation | async-start | bytes 786432 | tf_op jit(solution)/shard_map/all_to_all | solution.py:345
